TPU v7x, 256 devices: a whole 4x4x8 slice. The times are simulated.
256 devices in a mesh: seq: 64 (over y_lo, x, z), tensor: 4 (over y_hi, core).
Axes of the slice: x: 4, y: 4 (y_hi: 2, y_lo: 2; y = y_hi * 2 + y_lo), z: 8, core: 2. Of those that a mesh axis runs over, the one named last changes fastest.
Arguments:
- tokens: bfloat16 [32768, 2048], P('seq', 'tensor'), may hold values from -12 to 12
- attn_gain: float32 [2048], replicated, may hold values from 0.1 to 1.9
- w_query: bfloat16 [2048, 2048], P('seq', 'tensor'), as said below
- w_key: bfloat16 [2048, 512], P('seq', 'tensor'), as said below
- w_value: bfloat16 [2048, 512], P('seq', 'tensor'), may hold values from -0.125 to 0.125
- w_out: bfloat16 [2048, 2048], P('tensor', 'seq'), may hold values from -0.125 to 0.125
- mlp_gain: float32 [2048], replicated, may hold values from 0.1 to 1.9
- w_gate: bfloat16 [2048, 5632], P('seq', 'tensor'), may hold values from -0.125 to 0.125
- w_up: bfloat16 [2048, 5632], P('seq', 'tensor'), may hold values from -0.125 to 0.125
- w_down: bfloat16 [5632, 2048], P('tensor', 'seq'), may hold values from -0.078125 to 0.078125
Outputs:
- layer_out: bfloat16 [32768, 2048], P('seq', 'tensor')
Inputs may be any that keep to these rules, and one draw needn't show every extreme that they name: `w_query`: entries are of order 2048 to the power -1/2. `w_key`: entries are of order 2048 to the power -1/2.
All inputs are finite; a program needn't handle non-finite values.
Results may differ from a plain program's by a relative error of at most 0.013.
Values may be sent and summed in bfloat16 or wider, within the bound.
No kernel may reach another device: no remote copies, remote signals or barrier semaphores. Data moves between devices by JAX's collectives and lax.ppermute only.
A program may use at most 128 MiB of HBM per device.

v0:
```python
import jax
import jax.numpy as jnp
from jax import lax
from jax.sharding import Mesh
from jax.sharding import PartitionSpec as P

HEAD_DIM = 128
WINDOW = 1024
SEQ = ("seq_0", "seq_1", "seq_2")


def copy_for_each(value, axis):
    length = lax.axis_size(axis)
    return lax.all_to_all(
        jnp.broadcast_to(value[None], (length, *value.shape)), axis, 0, 0, tiled=True
    )


def in_order(tiles, dim):
    tiles = jnp.moveaxis(tiles, 0, dim)
    shape = tiles.shape
    return tiles.reshape(*shape[:dim], shape[dim] * shape[dim + 1], *shape[dim + 2 :])


def gathered_copies(value, axis, dim):
    tiles = copy_for_each(value, axis)
    return in_order(tiles, dim)


def sent_together(arrays, axis, dim, along):
    ends, at = ([], 0)
    for a in arrays[:-1]:
        at += a.shape[along]
        ends.append(at)
    both = jnp.concatenate(arrays, axis=along)
    return tuple(jnp.split(lax.all_gather(both, axis, axis=dim, tiled=True), ends, axis=along))


def passed_along(block, axis, distance):
    devices = range(lax.axis_size(axis))
    route = [(i - distance, i) for i in devices if i - distance in devices]
    return lax.ppermute(block, axis, route)


def in_blocks(value, dim, length):
    shape = value.shape
    tiles = value.reshape(*shape[:dim], length, shape[dim] // length, *shape[dim + 1 :])
    return jnp.moveaxis(tiles, dim, 0)


def sent_and_summed(value, axis, dim):
    length = lax.axis_size(axis)
    tiles = lax.all_to_all(in_blocks(value, dim, length), axis, 0, 0, tiled=True)
    return jnp.sum(tiles.astype(jnp.float32), axis=0)


def all_blocks(value, axes, sequence):
    tiles = value[None]
    for k in sequence:
        tiles = lax.all_gather(tiles, axes[k], axis=0, tiled=True)
    carried = [lax.axis_size(axes[k]) for k in reversed(sequence)]
    tiles = tiles.reshape(*carried, *value.shape)
    turned = sorted(range(len(sequence)), key=lambda place: sequence[len(sequence) - 1 - place])
    return tiles.transpose(*turned, *range(len(sequence), tiles.ndim)).reshape(-1, *value.shape)


def gather_axes(value, axes, sequence, dim):
    return in_order(all_blocks(value, axes, sequence), dim)


def scaled_rows(values, gain):
    values = values.astype(jnp.float32)
    mean_square = jnp.mean(values * values, axis=1, keepdims=True)
    return (values * lax.rsqrt(mean_square + 1e-06) * gain).astype(jnp.bfloat16)


def product(left, right):
    return jnp.dot(left, right, preferred_element_type=jnp.float32)


def window_attention(queries, context_keys, context_values, reach, position):
    rows = queries.shape[0]
    local_kv = context_keys.shape[1] // HEAD_DIM
    group = queries.shape[1] // (local_kv * HEAD_DIM)
    block = min(512, rows)
    span = WINDOW + block
    scale = HEAD_DIM ** (-0.5)
    start = reach * rows - WINDOW
    query_block = queries.reshape(block, local_kv, group, HEAD_DIM)
    key_block = context_keys.reshape(span, local_kv, HEAD_DIM)
    value_block = context_values.reshape(span, local_kv, HEAD_DIM)
    scores = (
        jnp.einsum("qkgd,ckd->kgqc", query_block, key_block, preferred_element_type=jnp.float32)
        * scale
    )
    query_pos = lax.broadcasted_iota(jnp.int32, (block, span), 0)
    key_pos = lax.broadcasted_iota(jnp.int32, (block, span), 1)
    distance = query_pos + WINDOW - key_pos
    first_key = (position - reach) * rows + start
    allowed = (distance >= 0) & (distance < WINDOW) & (key_pos + first_key >= 0)
    scores = jnp.where(allowed[None, None], scores, -1e30)
    highest = jnp.max(scores, axis=3, keepdims=True)
    raised = jnp.exp(scores - highest)
    weights = (raised / jnp.sum(raised, axis=3, keepdims=True)).astype(jnp.bfloat16)
    mixed = jnp.einsum("kgqc,ckd->qkgd", weights, value_block, preferred_element_type=jnp.float32)
    outputs = mixed.astype(jnp.bfloat16).reshape(block, local_kv * group * HEAD_DIM)
    return outputs


def per_device(tokens, attn_gain, w_query, w_key, w_value, w_out, mlp_gain, w_gate, w_up, w_down):
    rows = tokens.shape[0]
    whole = gathered_copies(tokens, "tensor", 1)
    normed = scaled_rows(whole, attn_gain)
    query_full, key_full, value_full = sent_together((w_query, w_key, w_value), SEQ, 0, 1)
    queries = product(normed, query_full).astype(jnp.bfloat16)
    keys = product(normed, key_full).astype(jnp.bfloat16)
    values = product(normed, value_full).astype(jnp.bfloat16)
    reach = -(-WINDOW // rows)
    earlier = []
    current = (keys, values)
    for step in range(reach):
        current = passed_along((current[0], current[1]), SEQ, 1)
        earlier.append(current)
    context_keys = jnp.concatenate(
        [earlier[reach - 1 - step][0] for step in range(reach)] + [keys], axis=0
    )
    context_values = jnp.concatenate(
        [earlier[reach - 1 - step][1] for step in range(reach)] + [values], axis=0
    )
    position = lax.axis_index(SEQ)
    attended = window_attention(queries, context_keys, context_values, reach, position)
    out_full = gathered_copies(w_out, SEQ, 1)
    head_terms = product(attended, out_full)
    attn_share = sent_and_summed(head_terms.astype(jnp.bfloat16), "tensor", 1)
    stream_share = (tokens.astype(jnp.float32) + attn_share).astype(jnp.bfloat16)
    stream_whole = gathered_copies(stream_share, "tensor", 1)
    stream_normed = scaled_rows(stream_whole, mlp_gain)
    gate_full, up_full = sent_together((w_gate, w_up), SEQ, 0, 1)
    gate = product(stream_normed, gate_full)
    upward = product(stream_normed, up_full)
    hidden = (jax.nn.silu(gate) * upward).astype(jnp.bfloat16)
    down_full = gather_axes(w_down, SEQ, (0, 1, 2), 1)
    unit_terms = product(hidden, down_full)
    mlp_share = sent_and_summed(unit_terms.astype(jnp.bfloat16), "tensor", 1)
    return (stream_share.astype(jnp.float32) + mlp_share).astype(jnp.bfloat16)


def solution(mesh):
    split = Mesh(
        mesh.devices.reshape(2, 4, 8, mesh.shape["tensor"]), ("seq_0", "seq_1", "seq_2", "tensor")
    )
    placed = (
        P(SEQ, "tensor"),
        P(),
        P(SEQ, "tensor"),
        P(SEQ, "tensor"),
        P(SEQ, "tensor"),
        P("tensor", SEQ),
        P(),
        P(SEQ, "tensor"),
        P(SEQ, "tensor"),
        P("tensor", SEQ),
    )
    return jax.shard_map(
        per_device, mesh=split, in_specs=placed, out_specs=P(SEQ, "tensor"), check_vma=False
    )
```

profile of v0, /device:TPU:1, one launch (start us, length us, event | category | flops | bytes accessed | tf_op | source)
XLA Modules:
  0.0 769.3 jit_solution(572772055486221659)
XLA Ops:
  8.1 5.0 all-gather
  13.1 13.0 %all_gather.18 = bf16[8,1408,32]{1,2,0:T(8,128)(2,1)} all-gather(bf16[2,1408,32]{1,2,0:T(8,128)(2,1)S(1)} %bitcast.99), channel_id=1, replica_groups=mesh['seq_0'=2,'seq_1'=4,'seq_2'=8,'tensor'=4] {'seq_1'}, dimensions={0}, use_global_device_ids=true | all-gather | bytes 901120 | tf_op jit(solution)/shard_map/all_gather | solution.py:60
  26.1 1.6 pad_maximum_fusion
  29.5 9.4 %all-to-all-start = ((bf16[4,512,512]{1,2,0:T(8,128)(2,1)}), bf16[4,512,512]{1,2,0:T(8,128)(2,1)S(1)}, u32[]{:S(2)}, u32[]{:S(2)}) async-start(bf16[4,512,512]{1,2,0:T(8,128)(2,1)} %broadcast_in_dim.20), calls=%async_computation | async-start | bytes 4194304 | tf_op jit(solution)/shard_map/all_to_all | solution.py:14
  40.2 28.7 %all-to-all-done = bf16[4,512,512]{1,2,0:T(8,128)(2,1)S(1)} async-done(((bf16[4,512,512]{1,2,0:T(8,128)(2,1)}), bf16[4,512,512]{1,2,0:T(8,128)(2,1)S(1)}, u32[]{:S(2)}, u32[]{:S(2)}) %all-to-all-start) | async-done | bytes 2097184 | tf_op jit(solution)/shard_map/all_to_all | solution.py:14
  70.5 9.6 %all-to-all-start.1 = ((bf16[64,512,32]{1,2,0:T(8,128)(2,1)}), bf16[64,512,32]{1,2,0:T(8,128)(2,1)}, u32[]{:S(2)}, u32[]{:S(2)}) async-start(bf16[64,512,32]{1,2,0:T(8,128)(2,1)} %broadcast_in_dim.23), calls=%async_computation.1 | async-start | bytes 4194304 | tf_op jit(solution)/shard_map/all_to_all | solution.py:14
  80.6 1.9 fusion.11
  82.6 194.5 %all-gather.5.cloned.1.call-done = bf16[2048,768]{1,0:T(8,128)(2,1)} async-done(((bf16[32,768]{1,0:T(8,128)(2,1)}), bf16[2048,768]{1,0:T(8,128)(2,1)}) %all-gather.5.cloned.1.call-update) | async-done | bytes 3145744 | tf_op jit(solution)/shard_map/all_gather | solution.py:36
  277.0 2.6 convolution_convert_fusion.2
  280.9 2.4 convolution_convert_fusion.3
  283.4 1.8 collective-permute-start
  285.2 1.9 collective-permute-start.3
  288.5 3.1 collective-permute-start.1
  291.6 2.4 fusion.1
  294.0 2.8 fusion
  296.8 4.1 fusion.27
  300.8 2.9 convolution_convert_fusion
  303.9 79.6 %all_to_all.25 = bf16[4,512,512]{2,1,0:T(8,128)(2,1)S(1)} all-to-all(bf16[4,512,512]{2,1,0:T(8,128)(2,1)S(1)} %bitcast.93), channel_id=1, replica_groups=mesh['seq_0'=2,'seq_1'=4,'seq_2'=8,'tensor'=4] {'tensor'}, dimensions={0} | all-to-all | bytes 4194304 | tf_op jit(solution)/shard_map/all_to_all | solution.py:53
  384.4 34.1 %all_to_all.26 = bf16[4,512,512]{1,2,0:T(8,128)(2,1)S(1)} all-to-all(bf16[4,512,512]{1,2,0:T(8,128)(2,1)S(1)} %broadcast_in_dim.24), channel_id=1, replica_groups=mesh['seq_0'=2,'seq_1'=4,'seq_2'=8,'tensor'=4] {'tensor'}, dimensions={0} | all-to-all | bytes 4194304 | tf_op jit(solution)/shard_map/all_to_all | solution.py:14
  419.6 6.5 copy.49
  426.1 241.3 %all-gather.7.cloned.1.call-done = bf16[2048,2816]{1,0:T(8,128)(2,1)} async-done(((bf16[32,2816]{1,0:T(8,128)(2,1)}), bf16[2048,2816]{1,0:T(8,128)(2,1)}) %all-gather.7.cloned.1.call-update) | async-done | bytes 11534352 | tf_op jit(solution)/shard_map/all_gather | solution.py:36
  667.5 7.7 %fusion.6 = f32[512,1408]{1,0:T(8,128)} fusion(bf16[512,2048]{0,1:T(8,128)(2,1)S(1)} %fusion.9, bf16[2048,2816]{1,0:T(8,128)(2,1)} %all-gather.7.cloned.1.call-done), kind=kOutput, calls=%fused_computation.9 | convolution fusion | flops 2952790016 | bytes 10747904 | tf_op jit(solution)/shard_map/dot_general | solution.py:78
  675.2 12.8 %convolution_convert_fusion.1 = bf16[512,2048]{1,0:T(8,128)(2,1)S(1)} fusion(bf16[1408,2048]{0,1:T(8,128)(2,1)} %bitcast.96, bf16[512,2048]{0,1:T(8,128)(2,1)} %copy-done.1, bf16[2048,2816]{1,0:T(8,128)(2,1)} %all-gather.7.cloned.1.call-done, f32[512,1408]{1,0:T(8,128)} %fusion.6), kind=kOutput, calls=%fused_computation.29 | convolution fusion | flops 5910953984 | bytes 18612224 | tf_op jit(solution)/shard_map/dot_general | solution.py:78
  688.2 73.2 %all_to_all.27 = bf16[4,512,512]{2,1,0:T(8,128)(2,1)S(1)} all-to-all(bf16[4,512,512]{2,1,0:T(8,128)(2,1)S(1)} %bitcast.94), channel_id=1, replica_groups=mesh['seq_0'=2,'seq_1'=4,'seq_2'=8,'tensor'=4] {'tensor'}, dimensions={0} | all-to-all | bytes 4194304 | tf_op jit(solution)/shard_map/all_to_all | solution.py:53
  (49 shorter events, 12.9 us)
Async XLA Ops:
  6.5 21.2 %copy-start.2 = (bf16[512,512]{1,0:T(8,128)(2,1)S(1)}, bf16[512,512]{1,0:T(8,128)(2,1)}, u32[]{:S(2)}) copy-start(bf16[512,512]{1,0:T(8,128)(2,1)} %param.10) | copy-start | bytes 1572868
  6.5 270.5 %all-gather.5.cloned.1.call-start = ((), (), s32[]{:S(2)}) async-start(), calls=%async_computation.5 | async-start | bytes 3194880 | tf_op jit(solution)/shard_map/all_gather | solution.py:36
  8.0 411.6 %all-gather.9.cloned.1.call-start = ((), (), s32[]{:S(2)}) async-start(), calls=%async_computation.7 | async-start | bytes 6488064 | tf_op jit(solution)/shard_map/all_gather | solution.py:60
  26.1 641.4 %all-gather.7.cloned.1.call-start = ((), (), s32[]{:S(2)}) async-start(), calls=%async_computation.6 | async-start | bytes 11714560 | tf_op jit(solution)/shard_map/all_gather | solution.py:36
  29.5 39.5 %copy-start.3 = (bf16[512,32]{0,1:T(8,128)(2,1)S(1)}, bf16[512,32]{0,1:T(8,128)(2,1)}, u32[]{:S(2)}) copy-start(bf16[512,32]{0,1:T(8,128)(2,1)} %param.15) | copy-start | bytes 98308
  29.5 39.5 %all-to-all-start = ((bf16[4,512,512]{1,2,0:T(8,128)(2,1)}), bf16[4,512,512]{1,2,0:T(8,128)(2,1)S(1)}, u32[]{:S(2)}, u32[]{:S(2)}) async-start(bf16[4,512,512]{1,2,0:T(8,128)(2,1)} %broadcast_in_dim.20), calls=%async_computation | async-start | bytes 4194304 | tf_op jit(solution)/shard_map/all_to_all | solution.py:14
  70.5 10.1 %copy-start.4 = (f32[2048]{0:T(1024)S(1)}, f32[2048]{0:T(1024)}, u32[]{:S(2)}) copy-start(f32[2048]{0:T(1024)} %param.11) | copy-start | bytes 24580
  70.5 230.3 %all-to-all-start.1 = ((bf16[64,512,32]{1,2,0:T(8,128)(2,1)}), bf16[64,512,32]{1,2,0:T(8,128)(2,1)}, u32[]{:S(2)}, u32[]{:S(2)}) async-start(bf16[64,512,32]{1,2,0:T(8,128)(2,1)} %broadcast_in_dim.23), calls=%async_computation.1 | async-start | bytes 4194304 | tf_op jit(solution)/shard_map/all_to_all | solution.py:14
  82.6 204.6 %copy-start = (bf16[512,2048]{0,1:T(8,128)(2,1)S(1)}, bf16[512,2048]{0,1:T(8,128)(2,1)}, u32[]{:S(2)}) copy-start(bf16[512,2048]{0,1:T(8,128)(2,1)} %fusion.11) | copy-start | bytes 6291460
  277.0 10.1 %copy-start.6 = (bf16[2048,768]{1,0:T(8,128)(2,1)S(1)}, bf16[2048,768]{1,0:T(8,128)(2,1)}, u32[]{:S(2)}) copy-start(bf16[2048,768]{1,0:T(8,128)(2,1)} %all-gather.5.cloned.1.call-done) | copy-start | bytes 9437188
  279.6 5.6 collective-permute-start.2
  283.4 5.1 collective-permute-start
  285.2 6.4 collective-permute-start.3
  288.5 8.3 %collective-permute-start.1 = (bf16[512,128]{1,0:T(8,128)(2,1)S(1)}, bf16[512,128]{1,0:T(8,128)(2,1)S(1)}, u32[]{:S(2)}, u32[]{:S(2)}) collective-permute-start(bf16[512,128]{1,0:T(8,128)(2,1)S(1)} %collective-permute-done), channel_id=1, source_target_pairs={{0,4},{4,8},{8,12},{12,16},{16,20},{20,24},{24,28},{28,32},{32,36}... | collective-permute-start | bytes 393224 | tf_op jit(solution)/shard_map/ppermute | solution.py:42
  384.4 34.6 %copy-start.5 = (f32[2048]{0:T(1024)S(1)}, f32[2048]{0:T(1024)}, u32[]{:S(2)}) copy-start(f32[2048]{0:T(1024)} %param.16) | copy-start | bytes 24580
  419.6 247.9 %copy-start.1 = (bf16[512,2048]{0,1:T(8,128)(2,1)}, bf16[512,2048]{0,1:T(8,128)(2,1)S(1)}, u32[]{:S(2)}) copy-start(bf16[512,2048]{0,1:T(8,128)(2,1)S(1)} %fusion.9) | copy-start | bytes 6291460
Sparse Core Ops, SparseCore 0:
  9.1 267.8 all-gather.4
  278.8 110.4 all-gather.8
  391.1 276.3 all-gather.6
where the time goes:
time: 770 us; the launch traced here: 769 us
  waiting for transfers between devices  465 us (60%)
  blocking collectives  205 us (27%)
  matrix products  36.2 us (5%)
  starting transfers between devices  27.3 us (4%)
  between operations  13.4 us (2%)
  other arithmetic  12.4 us (2%)
  local copies, waits for them, and re-layouts  10.6 us (1%)
    all_gather x2, waiting for transfers between devices, sent_together(): lax.all_gather(both, axis, axis=dim, tiled=True)  436 us
    all_to_all x2, blocking collectives, sent_and_summed(): lax.all_to_all(in_blocks(value, dim, length), axis, 0, 0, tiled=True)  153 us
    all_to_all x1, blocking collectives, copy_for_each(): lax.all_to_all(jnp.broadcast_to(value[None], (length, *value.shape)), axi...  34.1 us
    dot_general x6, matrix products, product(): return jnp.dot(left, right, preferred_element_type=jnp.float32)  29.8 us
    all_to_all x2, waiting for transfers between devices, copy_for_each(): lax.all_to_all(jnp.broadcast_to(value[None], (length, *value.shape)), axi...  28.7 us
    all_to_all x2, starting transfers between devices, copy_for_each(): lax.all_to_all(jnp.broadcast_to(value[None], (length, *value.shape)), axi...  19 us
    all_gather x2, blocking collectives, all_blocks(): tiles = lax.all_gather(tiles, axes[k], axis=0, tiled=True)  17.9 us
  transfers between devices with their start and end apart: 9, of which 3 were waited for; matrix products, arithmetic and copies ran while one was open for 5% of the time, Pallas kernels for 0%

commit v1 on v0

--- a/solution.py
+++ b/solution.py
@@ -57,7 +57,8 @@
 def all_blocks(value, axes, sequence):
     tiles = value[None]
     for k in sequence:
-        tiles = lax.all_gather(tiles, axes[k], axis=0, tiled=True)
+        outgoing = jnp.stack([tiles] * lax.axis_size(axes[k]))
+        tiles = jnp.concatenate(lax.all_to_all(outgoing, axes[k], 0, 0), axis=0)
     carried = [lax.axis_size(axes[k]) for k in reversed(sequence)]
     tiles = tiles.reshape(*carried, *value.shape)
     turned = sorted(range(len(sequence)), key=lambda place: sequence[len(sequence) - 1 - place])

time: 770 us -> 763 us (level)
  waiting for transfers between devices: 465 us -> 430 us
  starting transfers between devices: 27.3 us -> 45.1 us
    all_gather x2, waiting for transfers between devices: 436 us -> 218 us  [sent_together(): lax.all_gather(both, axis, axis=dim, tiled=True)]
    all_to_all x0 -> x3, waiting for transfers between devices: none -> 186 us  [all_blocks(): tiles = jnp.concatenate(lax.all_to_all(outgoing, axes[k], 0, 0), axis=0)]
    all_to_all x0 -> x3, starting transfers between devices: none -> 18.4 us  [all_blocks(): tiles = jnp.concatenate(lax.all_to_all(outgoing, axes[k], 0, 0), axis=0)]
    all_gather x2 -> x0, blocking collectives: 17.9 us -> none  [all_blocks(): tiles = lax.all_gather(tiles, axes[k], axis=0, tiled=True)]
    all_to_all x1, blocking collectives: 34.1 us -> 47.4 us  [copy_for_each(): lax.all_to_all(jnp.broadcast_to(value[None], (length, *value.shape)), axi...]
  transfers between devices with their start and end apart: 9 -> 11, of which waited for: 3 -> 6; matrix products, arithmetic and copies ran while one was open for 5% -> 6% of each run, Pallas kernels for 0% -> 0%
where the time goes in v1:
time: 763 us; the launch traced here: 762 us
  waiting for transfers between devices  430 us (56%)
  blocking collectives  206 us (27%)
  starting transfers between devices  45.1 us (6%)
  matrix products  36.1 us (5%)
  local copies, waits for them, and re-layouts  16.3 us (2%)
  other arithmetic  15.4 us (2%)
  between operations  13.6 us (2%)
    all_gather x2, waiting for transfers between devices, sent_together(): lax.all_gather(both, axis, axis=dim, tiled=True)  218 us
    all_to_all x3, waiting for transfers between devices, all_blocks(): tiles = jnp.concatenate(lax.all_to_all(outgoing, axes[k], 0, 0), axis=0)  186 us
    all_to_all x2, blocking collectives, sent_and_summed(): lax.all_to_all(in_blocks(value, dim, length), axis, 0, 0, tiled=True)  159 us
    all_to_all x1, blocking collectives, copy_for_each(): lax.all_to_all(jnp.broadcast_to(value[None], (length, *value.shape)), axi...  47.4 us
    dot_general x6, matrix products, product(): return jnp.dot(left, right, preferred_element_type=jnp.float32)  29.6 us
    all_to_all x2, waiting for transfers between devices, copy_for_each(): lax.all_to_all(jnp.broadcast_to(value[None], (length, *value.shape)), axi...  26.6 us
    all_to_all x3, starting transfers between devices, all_blocks(): tiles = jnp.concatenate(lax.all_to_all(outgoing, axes[k], 0, 0), axis=0)  18.4 us
    all_to_all x2, starting transfers between devices, copy_for_each(): lax.all_to_all(jnp.broadcast_to(value[None], (length, *value.shape)), axi...  17.2 us
  transfers between devices with their start and end apart: 11, of which 6 were waited for; matrix products, arithmetic and copies ran while one was open for 6% of the time, Pallas kernels for 0%

profile of v1, /device:TPU:1, one launch (start us, length us, event | category | flops | bytes accessed | tf_op | source)
XLA Modules:
  0.0 762.3 jit_solution(11427931851733492878)
XLA Ops:
  12.4 6.9 all-to-all-start
  21.3 26.6 %all-to-all-done = bf16[4,512,512]{1,2,0:T(8,128)(2,1)S(1)} async-done(((bf16[4,512,512]{1,2,0:T(8,128)(2,1)}), bf16[4,512,512]{1,2,0:T(8,128)(2,1)S(1)}, u32[]{:S(2)}, u32[]{:S(2)}) %all-to-all-start) | async-done | bytes 2097184 | tf_op jit(solution)/shard_map/all_to_all | solution.py:14
  49.5 10.3 %all-to-all-start.1 = ((bf16[64,512,32]{1,2,0:T(8,128)(2,1)}), bf16[64,512,32]{1,2,0:T(8,128)(2,1)}, u32[]{:S(2)}, u32[]{:S(2)}) async-start(bf16[64,512,32]{1,2,0:T(8,128)(2,1)} %broadcast_in_dim.21), calls=%async_computation.1 | async-start | bytes 4194304 | tf_op jit(solution)/shard_map/all_to_all | solution.py:14
  62.2 215.2 %all-gather.3.cloned.1.call-done = bf16[2048,768]{1,0:T(8,128)(2,1)} async-done(((bf16[32,768]{1,0:T(8,128)(2,1)}), bf16[2048,768]{1,0:T(8,128)(2,1)}) %all-gather.3.cloned.1.call-update) | async-done | bytes 3145744 | tf_op jit(solution)/shard_map/all_gather | solution.py:36
  277.4 2.6 convolution_convert_fusion.2
  280.0 2.5 collective-permute-start.2
  282.5 2.4 convolution_convert_fusion.3
  290.1 3.1 collective-permute-start.1
  295.6 2.8 fusion
  298.4 4.1 fusion.27
  302.5 9.8 %all-to-all-start.4 = ((bf16[2,1,1408,32]{2,3,1,0:T(8,128)(2,1)}), bf16[2,1,1408,32]{2,3,1,0:T(8,128)(2,1)S(1)}, u32[]{:S(2)}, u32[]{:S(2)}) async-start(bf16[2,1,1408,32]{2,3,1,0:T(8,128)(2,1)} %pad_maximum_fusion.1), calls=%async_computation.4 | async-start | bytes 360448 | tf_op jit(solution)/shard_map/all_to_all | solution.py:61
  312.3 2.9 convolution_convert_fusion
  317.0 97.5 %all_to_all.40 = bf16[4,512,512]{2,1,0:T(8,128)(2,1)S(1)} all-to-all(bf16[4,512,512]{2,1,0:T(8,128)(2,1)} %bitcast.92), channel_id=1, replica_groups=mesh['seq_0'=2,'seq_1'=4,'seq_2'=8,'tensor'=4] {'tensor'}, dimensions={0} | all-to-all | bytes 4194304 | tf_op jit(solution)/shard_map/all_to_all | solution.py:53
  415.5 3.5 all-to-all-start.5
  420.7 15.9 %all-to-all-done.5 = bf16[4,2,1408,32]{2,3,1,0:T(8,128)(2,1)S(1)} async-done(((bf16[4,2,1408,32]{2,3,1,0:T(8,128)(2,1)}), bf16[4,2,1408,32]{2,3,1,0:T(8,128)(2,1)S(1)}, u32[]{:S(2)}, u32[]{:S(2)}) %all-to-all-start.5) | async-done | bytes 720928 | tf_op jit(solution)/shard_map/all_to_all | solution.py:61
  436.8 47.4 %all_to_all.41 = bf16[4,512,512]{1,2,0:T(8,128)(2,1)S(1)} all-to-all(bf16[4,512,512]{1,2,0:T(8,128)(2,1)S(1)} %broadcast_in_dim.22), channel_id=1, replica_groups=mesh['seq_0'=2,'seq_1'=4,'seq_2'=8,'tensor'=4] {'tensor'}, dimensions={0} | all-to-all | bytes 4194304 | tf_op jit(solution)/shard_map/all_to_all | solution.py:14
  484.2 3.0 stack.11
  487.2 5.0 all-to-all-start.6
  494.7 169.4 %all-to-all-done.6 = bf16[8,8,1408,32]{2,3,1,0:T(8,128)(2,1)} async-done(((bf16[8,8,1408,32]{2,3,1,0:T(8,128)(2,1)}), bf16[8,8,1408,32]{2,3,1,0:T(8,128)(2,1)}, u32[]{:S(2)}, u32[]{:S(2)}) %all-to-all-start.6) | async-done | bytes 5767200 | tf_op jit(solution)/shard_map/all_to_all | solution.py:61
  664.1 5.9 copy.34
  670.0 2.6 all-gather.5.cloned.1.call-done
  672.5 7.6 %fusion.6 = f32[512,1408]{1,0:T(8,128)} fusion(bf16[512,2048]{0,1:T(8,128)(2,1)S(1)} %copy-done.1, bf16[2048,2816]{1,0:T(8,128)(2,1)} %all-gather.5.cloned.1.call-done), kind=kOutput, calls=%fused_computation.9 | convolution fusion | flops 2952790016 | bytes 10747904 | tf_op jit(solution)/shard_map/dot_general | solution.py:79
  680.2 12.8 %convolution_convert_fusion.1 = bf16[512,2048]{1,0:T(8,128)(2,1)S(1)} fusion(bf16[1408,2048]{0,1:T(8,128)(2,1)} %bitcast.94, bf16[512,2048]{0,1:T(8,128)(2,1)} %fusion.9, bf16[2048,2816]{1,0:T(8,128)(2,1)} %all-gather.5.cloned.1.call-done, f32[512,1408]{1,0:T(8,128)} %fusion.6), kind=kOutput, calls=%fused_computation.29 | convolution fusion | flops 5910953984 | bytes 18612224 | tf_op jit(solution)/shard_map/dot_general | solution.py:79
  693.2 61.0 %all_to_all.42 = bf16[4,512,512]{2,1,0:T(8,128)(2,1)S(1)} all-to-all(bf16[4,512,512]{2,1,0:T(8,128)(2,1)S(1)} %bitcast.93), channel_id=1, replica_groups=mesh['seq_0'=2,'seq_1'=4,'seq_2'=8,'tensor'=4] {'tensor'}, dimensions={0} | all-to-all | bytes 4194304 | tf_op jit(solution)/shard_map/all_to_all | solution.py:53
  (52 shorter events, 27.8 us)
Async XLA Ops:
  6.5 270.8 %all-gather.3.cloned.1.call-start = ((), (), s32[]{:S(2)}) async-start(), calls=%async_computation.8 | async-start | bytes 3194880 | tf_op jit(solution)/shard_map/all_gather | solution.py:36
  8.0 664.6 %all-gather.5.cloned.1.call-start = ((), (), s32[]{:S(2)}) async-start(), calls=%async_computation.9 | async-start | bytes 11714560 | tf_op jit(solution)/shard_map/all_gather | solution.py:36
  10.9 8.4 %copy-start.2 = (bf16[1408,32]{0,1:T(8,128)(2,1)S(1)}, bf16[1408,32]{0,1:T(8,128)(2,1)}, u32[]{:S(2)}) copy-start(bf16[1408,32]{0,1:T(8,128)(2,1)} %param.19) | copy-start | bytes 270340
  12.4 35.5 %copy-start.3 = (bf16[512,32]{0,1:T(8,128)(2,1)S(1)}, bf16[512,32]{0,1:T(8,128)(2,1)}, u32[]{:S(2)}) copy-start(bf16[512,32]{0,1:T(8,128)(2,1)} %param.15) | copy-start | bytes 98308
  12.4 35.5 %all-to-all-start = ((bf16[4,512,512]{1,2,0:T(8,128)(2,1)}), bf16[4,512,512]{1,2,0:T(8,128)(2,1)S(1)}, u32[]{:S(2)}, u32[]{:S(2)}) async-start(bf16[4,512,512]{1,2,0:T(8,128)(2,1)} %broadcast_in_dim.18), calls=%async_computation | async-start | bytes 4194304 | tf_op jit(solution)/shard_map/all_to_all | solution.py:14
  49.5 10.8 %copy-start.4 = (f32[2048]{0:T(1024)S(1)}, f32[2048]{0:T(1024)}, u32[]{:S(2)}) copy-start(f32[2048]{0:T(1024)} %param.11) | copy-start | bytes 24580
  49.5 252.9 %all-to-all-start.1 = ((bf16[64,512,32]{1,2,0:T(8,128)(2,1)}), bf16[64,512,32]{1,2,0:T(8,128)(2,1)}, u32[]{:S(2)}, u32[]{:S(2)}) async-start(bf16[64,512,32]{1,2,0:T(8,128)(2,1)} %broadcast_in_dim.21), calls=%async_computation.1 | async-start | bytes 4194304 | tf_op jit(solution)/shard_map/all_to_all | solution.py:14
  62.2 226.6 %copy-start = (bf16[512,2048]{0,1:T(8,128)(2,1)S(1)}, bf16[512,2048]{0,1:T(8,128)(2,1)}, u32[]{:S(2)}) copy-start(bf16[512,2048]{0,1:T(8,128)(2,1)} %fusion.11) | copy-start | bytes 6291460
  277.4 11.4 %copy-start.6 = (bf16[2048,768]{1,0:T(8,128)(2,1)S(1)}, bf16[2048,768]{1,0:T(8,128)(2,1)}, u32[]{:S(2)}) copy-start(bf16[2048,768]{1,0:T(8,128)(2,1)} %all-gather.3.cloned.1.call-done) | copy-start | bytes 9437188
  280.0 6.9 collective-permute-start.2
  284.9 5.2 collective-permute-start
  286.9 6.4 collective-permute-start.3
  290.1 8.2 %collective-permute-start.1 = (bf16[512,128]{1,0:T(8,128)(2,1)S(1)}, bf16[512,128]{1,0:T(8,128)(2,1)S(1)}, u32[]{:S(2)}, u32[]{:S(2)}) collective-permute-start(bf16[512,128]{1,0:T(8,128)(2,1)S(1)} %collective-permute-done), channel_id=1, source_target_pairs={{0,4},{4,8},{8,12},{12,16},{16,20},{20,24},{24,28},{28,32},{32,36}... | collective-permute-start | bytes 393224 | tf_op jit(solution)/shard_map/ppermute | solution.py:42
  302.5 14.6 %all-to-all-start.4 = ((bf16[2,1,1408,32]{2,3,1,0:T(8,128)(2,1)}), bf16[2,1,1408,32]{2,3,1,0:T(8,128)(2,1)S(1)}, u32[]{:S(2)}, u32[]{:S(2)}) async-start(bf16[2,1,1408,32]{2,3,1,0:T(8,128)(2,1)} %pad_maximum_fusion.1), calls=%async_computation.4 | async-start | bytes 360448 | tf_op jit(solution)/shard_map/all_to_all | solution.py:61
  415.5 21.1 %all-to-all-start.5 = ((bf16[4,2,1408,32]{2,3,1,0:T(8,128)(2,1)}), bf16[4,2,1408,32]{2,3,1,0:T(8,128)(2,1)S(1)}, u32[]{:S(2)}, u32[]{:S(2)}) async-start(bf16[4,2,1408,32]{2,3,1,0:T(8,128)(2,1)} %stack.10), calls=%async_computation.5 | async-start | bytes 1441792 | tf_op jit(solution)/shard_map/all_to_all | solution.py:61
  487.2 5.6 copy-start.5
  487.2 176.9 %all-to-all-start.6 = ((bf16[8,8,1408,32]{2,3,1,0:T(8,128)(2,1)}), bf16[8,8,1408,32]{2,3,1,0:T(8,128)(2,1)}, u32[]{:S(2)}, u32[]{:S(2)}) async-start(bf16[8,8,1408,32]{2,3,1,0:T(8,128)(2,1)} %stack.11), calls=%async_computation.6 | async-start | bytes 11534336 | tf_op jit(solution)/shard_map/all_to_all | solution.py:61
  664.1 8.5 %copy-start.1 = (bf16[512,2048]{0,1:T(8,128)(2,1)S(1)}, bf16[512,2048]{0,1:T(8,128)(2,1)}, u32[]{:S(2)}) copy-start(bf16[512,2048]{0,1:T(8,128)(2,1)} %fusion.9) | copy-start | bytes 6291460
Sparse Core Ops, SparseCore 0:
  9.1 268.2 all-gather.2
  279.2 393.3 all-gather.4
